TPU v7x, 256 devices: a whole 4x4x8 slice. The times are simulated.
256 devices in a mesh: dp: 4 (over x), vocab: 64 (over y, z, core).
Axes of the slice: x: 4, y: 4, z: 8, core: 2. Of those that a mesh axis runs over, the one named last changes fastest.
Arguments:
- hidden: bfloat16 [1024, 8192], P('dp'), may hold values from -14 to 14
- weight: bfloat16 [8192, 65536], P('dp', 'vocab'), may hold values from -1 to 1, as said below
- targets: int32 [1024], P('dp'), may hold values from 0 to 65535
- cotangent: float32 [1024], P('dp'), may hold values from 1 to 8
Outputs:
- loss: float32 [1024], P('dp')
- grad_hidden: bfloat16 [1024, 8192], P('vocab', 'dp')
- grad_weight: bfloat16 [8192, 65536], P('dp', 'vocab')
Inputs may be any that keep to these rules, and one draw needn't show every extreme that they name: `weight`: entries drawn with standard deviation 4 / sqrt(8192).
All inputs are finite; a program needn't handle non-finite values.
Results may differ from a plain program's by a relative error of at most 0.0047.
Values may be sent and summed in bfloat16 or wider, within the bound.
A program may use at most 128 MiB of HBM per device.

v0:
```python
import jax
import jax.numpy as jnp
from jax import lax
from jax.sharding import PartitionSpec as P


def copy_for_each(shard, axis):
    peers = lax.axis_size(axis)
    return lax.all_to_all(
        jnp.broadcast_to(shard[None], (peers, *shard.shape)), axis, 0, 0, tiled=True
    )


def collected_together(shard, axis):
    leaves = jax.tree.leaves(shard)
    sequence = sorted(range(len(leaves)), key=lambda k: -leaves[k].size)
    width = (1, *leaves[sequence[0]].shape)[-1]
    lines = [
        jnp.pad(leaves[k].reshape(-1), (0, -leaves[k].size % width)).reshape(-1, width)
        for k in sequence
    ]
    both, at, found = (copy_for_each(jnp.concatenate(lines), axis), 0, {})
    for k, line in zip(sequence, lines):
        slab = both[:, at : at + len(line)].reshape(len(both), -1)
        found[k] = slab[:, : leaves[k].size].reshape(-1, *leaves[k].shape)
        at += len(line)
    numbers = iter(range(len(leaves)))
    return jax.tree.map(lambda _: found[next(numbers)], shard)


def combined_pairwise(pieces, combine):
    while len(jax.tree.leaves(pieces)[0]) > 1:
        pieces = jax.vmap(combine)(
            *(jax.tree.map(lambda part: part[side::2], pieces) for side in (0, 1))
        )
    return jax.tree.map(lambda part: part[0], pieces)


def joined_all(shard, axis, combine):
    pieces = collected_together(shard, axis)
    return combined_pairwise(pieces, combine)


def joined_along(tiles, dim):
    tiles = jnp.moveaxis(tiles, 0, dim)
    shape = tiles.shape
    return tiles.reshape(*shape[:dim], shape[dim] * shape[dim + 1], *shape[dim + 2 :])


def gather_directly(shard, axis, dim):
    tiles = copy_for_each(shard, axis)
    return joined_along(tiles, dim)


def combine(left_part, right_part):
    joined = jnp.maximum(left_part[0], right_part[0])
    scaled = left_part[1] * jnp.exp(left_part[0] - joined) + right_part[1] * jnp.exp(
        right_part[0] - joined
    )
    return (joined, scaled, left_part[2] + right_part[2])


def shards(hidden, weight, targets, cotangent):
    vocab_width = weight.shape[1]
    spread = lax.all_to_all(hidden, "dp", split_axis=1, concat_axis=0, tiled=True)
    vocab_first = lax.axis_index("vocab") * vocab_width
    columns = vocab_first + lax.iota(jnp.int32, vocab_width)
    onehot = (targets[:, None] == columns[None, :]).astype(jnp.float32)
    row_block = spread
    logits = lax.psum_scatter(
        jnp.dot(row_block, weight, preferred_element_type=jnp.float32),
        "dp",
        scatter_dimension=0,
        tiled=True,
    )
    local_max = jnp.max(logits, axis=1)
    local_pick = jnp.sum(logits * onehot, axis=1)
    local_exp = jnp.exp(logits - local_max[:, None])
    row_max, sum_exp, picked = joined_all(
        (local_max, jnp.sum(local_exp, axis=1), local_pick), "vocab", combine
    )
    shifted = local_exp * jnp.exp(local_max - row_max)[:, None]
    loss = row_max + jnp.log(sum_exp) - picked
    grad_logits = (cotangent[:, None] * (shifted / sum_exp[:, None] - onehot)).astype(jnp.bfloat16)
    all_grads = gather_directly(grad_logits, "dp", 0)
    grad_weight = lax.dot_general(
        spread, all_grads, (((0,), (0,)), ((), ())), preferred_element_type=jnp.float32
    ).astype(jnp.bfloat16)
    row_block = all_grads
    grad_hidden = lax.psum_scatter(
        lax.dot_general(
            row_block, weight, (((1,), (1,)), ((), ())), preferred_element_type=jnp.float32
        ),
        "vocab",
        scatter_dimension=0,
        tiled=True,
    ).astype(jnp.bfloat16)
    return (loss, grad_hidden, grad_weight)


def solution(mesh):
    in_specs = (P("dp", None), P("dp", "vocab"), P("dp"), P("dp"))
    out_specs = (P("dp"), P("vocab", "dp"), P("dp", "vocab"))
    return jax.shard_map(shards, mesh=mesh, in_specs=in_specs, out_specs=out_specs, check_vma=False)
```

profile of v0, /device:TPU:1, one launch (start us, length us, event | category | flops | bytes accessed | tf_op | source)
XLA Modules:
  0.0 353.3 jit_solution(16613334132285796834)
XLA Ops:
  7.2 0.0 reduce-scatter.3.cloned.1.call-start
  7.2 6.4 %copy.10 = bf16[256,8192]{0,1:T(8,128)(2,1)} copy(bf16[256,8192]{1,0:T(8,128)(2,1)} %param.4) | data formatting | bytes 8388608 | tf_op args[0]
  13.6 6.3 %copy.11 = bf16[256,4,2048]{2,0,1:T(8,128)(2,1)} copy(bf16[256,4,2048]{0,2,1:T(8,128)(2,1)} %bitcast.33) | data formatting | bytes 8388608 | tf_op jit(solution)/shard_map/all_to_all | solution.py:65
  19.8 0.0 copy-start.4
  19.9 51.6 %all_to_all.29 = bf16[256,4,2048]{2,0,1:T(8,128)(2,1)S(1)} all-to-all(bf16[256,4,2048]{2,0,1:T(8,128)(2,1)} %copy.11), channel_id=1, replica_groups=mesh['dp'=4,'vocab'=64] {'dp'}, dimensions={1} | all-to-all | bytes 8388608 | tf_op jit(solution)/shard_map/all_to_all | solution.py:65
  71.4 0.0 copy-start.1
  71.4 2.0 copy-done.1
  73.4 0.0 copy-done.4
  73.4 6.0 %fusion.11 = f32[1024,1024]{1,0:T(8,128)} fusion(bf16[1024,2048]{1,0:T(8,128)(2,1)S(1)} %bitcast.34, bf16[2048,1024]{1,0:T(8,128)(2,1)S(1)} %copy-done.4), kind=kOutput, calls=%fused_computation.29 | convolution fusion | flops 4294967296 | bytes 12582912 | tf_op jit(solution)/shard_map/dot_general | solution.py:71
  79.4 0.0 copy-start.2
  79.4 0.0 copy-start.3
  79.4 0.0 reduce-scatter.3.cloned.1.call-update
  79.4 0.0 reduce-scatter.5.cloned.1.call-start
  79.5 53.1 %reduce-scatter.3.cloned.1.call-done = f32[256,1024]{1,0:T(8,128)} async-done(((f32[1024,1024]{1,0:T(8,128)}), f32[256,1024]{1,0:T(8,128)}) %reduce-scatter.3.cloned.1.call-update) | async-done | bytes 1048592 | tf_op jit(solution)/shard_map/reduce_scatter | solution.py:70
  132.6 0.0 copy-start
  132.6 1.4 reduce_max.9
  134.0 0.0 copy-done.2
  134.1 1.6 fusion.8
  135.7 22.5 %all_to_all.30 = f32[64,3,256]{2,1,0:T(4,128)S(1)} all-to-all(f32[64,3,256]{2,1,0:T(4,128)S(1)} %broadcast_in_dim.4), channel_id=1, replica_groups=mesh['dp'=4,'vocab'=64] {'vocab'}, dimensions={0} | all-to-all | bytes 393216 | tf_op jit(solution)/shard_map/all_to_all | solution.py:9
  158.2 0.1 fusion.10
  159.2 0.6 subtract_exponential_fusion.1
  159.8 0.0 copy-done.3
  159.8 0.0 copy-done
  159.8 0.4 fusion.7
  160.2 0.2 copy.13
  160.4 0.1 broadcast_in_dim.5
  160.5 28.4 %all_to_all.31 = bf16[4,256,1024]{1,2,0:T(8,128)(2,1)S(1)} all-to-all(bf16[4,256,1024]{1,2,0:T(8,128)(2,1)S(1)} %broadcast_in_dim.5), channel_id=1, replica_groups=mesh['dp'=4,'vocab'=64] {'dp'}, dimensions={0} | all-to-all | bytes 4194304 | tf_op jit(solution)/shard_map/all_to_all | solution.py:9
  188.9 2.4 copy.14
  191.3 10.6 %fusion.12 = f32[1024,2048]{1,0:T(8,128)} fusion(bf16[1024,1024]{1,0:T(8,128)(2,1)} %bitcast.35, bf16[2048,1024]{1,0:T(8,128)(2,1)} %param.5), kind=kOutput, calls=%fused_computation.30 | convolution fusion | flops 4294967296 | bytes 14680064 | tf_op jit(solution)/shard_map/dot_general | solution.py:91
  201.9 0.0 reduce-scatter.5.cloned.1.call-update
  201.9 8.2 %fusion.1 = bf16[2048,1024]{0,1:T(8,128)(2,1)} fusion(bf16[4,256,1024]{1,2,0:T(8,128)(2,1)S(1)} %all_to_all.31, bf16[256,4,2048]{2,0,1:T(8,128)(2,1)} %copy-done.1), kind=kOutput, calls=%fused_computation.2 | convolution fusion | flops 4297064448 | bytes 10485760 | tf_op jit(solution)/shard_map/dot_general | solution.py:86
  210.1 6.5 %copy.15 = bf16[2048,1024]{1,0:T(8,128)(2,1)} copy(bf16[2048,1024]{0,1:T(8,128)(2,1)} %fusion.1) | data formatting | bytes 8388608
  216.6 128.3 %reduce-scatter.5.cloned.1.call-done = f32[16,2048]{1,0:T(8,128)} async-done(((f32[1024,2048]{1,0:T(8,128)}), f32[16,2048]{1,0:T(8,128)}) %reduce-scatter.5.cloned.1.call-update) | async-done | bytes 131088 | tf_op jit(solution)/shard_map/reduce_scatter | solution.py:90
  344.9 1.5 convert_element_type.17
  (47 shorter events, 0.8 us)
Async XLA Ops:
  7.2 125.4 %reduce-scatter.3.cloned.1.call-start = ((), (), s32[]{:S(2)}) async-start(), calls=%async_computation.5 | async-start | bytes 5242880 | tf_op jit(solution)/shard_map/reduce_scatter | solution.py:70
  19.8 53.5 %copy-start.4 = (bf16[2048,1024]{1,0:T(8,128)(2,1)S(1)}, bf16[2048,1024]{1,0:T(8,128)(2,1)}, u32[]{:S(2)}) copy-start(bf16[2048,1024]{1,0:T(8,128)(2,1)} %param.5) | copy-start | bytes 12582916
  71.4 2.0 copy-start.1
  79.4 54.7 %copy-start.2 = (s32[256]{0:T(256)S(1)}, s32[256]{0:T(256)}, u32[]{:S(2)}) copy-start(s32[256]{0:T(256)} %param.6) | copy-start | bytes 3076
  79.4 80.4 %copy-start.3 = (f32[256]{0:T(256)S(1)}, f32[256]{0:T(256)}, u32[]{:S(2)}) copy-start(f32[256]{0:T(256)} %param.7) | copy-start | bytes 3076
  79.4 265.5 %reduce-scatter.5.cloned.1.call-start = ((), (), s32[]{:S(2)}) async-start(), calls=%async_computation.6 | async-start | bytes 8519680 | tf_op jit(solution)/shard_map/reduce_scatter | solution.py:90
  132.6 27.2 %copy-start = (f32[256,1024]{1,0:T(8,128)S(1)}, f32[256,1024]{1,0:T(8,128)}, u32[]{:S(2)}) copy-start(f32[256,1024]{1,0:T(8,128)} %reduce-scatter.3.cloned.1.call-done) | copy-start | bytes 3145732
Sparse Core Ops, SparseCore 0:
  79.5 53.0 reduce-scatter.2
  202.0 142.8 reduce-scatter.4
where the time goes:
time: 358 us; the launch traced here: 353 us
  waiting for transfers between devices  181 us (51%)
  blocking collectives  102 us (28%)
  matrix products  24.8 us (7%)
  local copies, waits for them, and re-layouts  24.5 us (7%)
  between operations  14.2 us (4%)
  other arithmetic  5.72 us (2%)
    reduce_scatter x1, waiting for transfers between devices, shards(): lax.psum_scatter(lax.dot_general(row_block, weight, (((1,), (1,)), ((), (...  128 us
    reduce_scatter x1, waiting for transfers between devices, shards(): lax.psum_scatter(jnp.dot(row_block, weight, preferred_element_type=jnp.fl...  53.1 us
    all_to_all x1, blocking collectives, shards(): lax.all_to_all(hidden, 'dp', split_axis=1, concat_axis=0, tiled=True)  51.6 us
    all_to_all x2, blocking collectives, copy_for_each(): lax.all_to_all(jnp.broadcast_to(shard[None], (peers, *shard.shape)), axis...  50.9 us
    unnamed x13, local copies, waits for them, and re-layouts  14.8 us
    dot_general x1, matrix products, shards(): lax.dot_general(row_block, weight, (((1,), (1,)), ((), ())), preferred_el...  10.6 us
    dot_general x1, matrix products, shards(): lax.dot_general(spread, all_grads, (((0,), (0,)), ((), ())), preferred_el...  8.21 us
  transfers between devices with their start and end apart: 2, of which 2 were waited for; matrix products, arithmetic and copies ran while one was open for 4% of the time, Pallas kernels for 0%

commit v1 on v0

v1 whole, which is shorter than its diff:
```python
import jax
import jax.numpy as jnp
from jax import lax
from jax.experimental import pallas as pl
from jax.experimental.pallas import tpu as pltpu
from jax.sharding import PartitionSpec as P

F32, BF16, I16 = jnp.float32, jnp.bfloat16, jnp.int16
NX, NY, NZ = 4, 4, 8
FINE = 64.0 / 0.6931471805599453
TOP = 32700.0
NEG = (((1,), (1,)), ((), ()))


def row_code(x):
    top = jnp.max(jnp.abs(x), axis=1, keepdims=True)
    return jnp.ceil(jnp.log(jnp.maximum(top, 1e-30)) * FINE)


def pack_tall(x, dst):
    rows, cols = x.shape
    k = row_code(x)
    inv = jnp.exp(k * (-1.0 / FINE)) * TOP
    for j in range(cols // 128):
        dst[j * rows : (j + 1) * rows, :] = jnp.round(x[:, j * 128 : (j + 1) * 128] * inv).astype(I16)
    line = jnp.broadcast_to(k, (rows, 128)).T[0:1, :]
    dst[cols // 128 * rows : cols // 128 * rows + 16, :] = jnp.broadcast_to(line, (16, 128)).astype(I16)


def unpack_tall(src, rows, cols):
    at = cols // 128 * rows
    line = src[at : at + 16, :].astype(F32)[0:1, :]
    k = jnp.broadcast_to(line, (rows, rows)).T
    scale = jnp.exp(k * (1.0 / FINE)) * (1.0 / TOP)
    return jnp.concatenate(
        [src[j * rows : (j + 1) * rows, :].astype(F32) * scale for j in range(cols // 128)], axis=1
    )


def pack_flat(x, dst):
    rows, cols = x.shape
    k = row_code(x)
    inv = jnp.exp(k * (-1.0 / FINE)) * TOP
    for j in range(cols // 128):
        dst[j * rows : (j + 1) * rows, :] = jnp.round(x[:, j * 128 : (j + 1) * 128] * inv).astype(I16)
    dst[cols // 128 * rows : (cols // 128 + 1) * rows, :] = jnp.broadcast_to(k, (rows, 128)).astype(I16)


def unpack_flat(src, rows, cols):
    at = cols // 128 * rows
    scale = jnp.exp(src[at : at + rows, :].astype(F32) * (1.0 / FINE)) * (1.0 / TOP)
    return jnp.concatenate(
        [src[j * rows : (j + 1) * rows, :].astype(F32) * scale for j in range(cols // 128)], axis=1
    )


def as_column(line):
    n = line.shape[1]
    return jnp.broadcast_to(line, (128, n)).T[:, 0:1]


def as_line(column):
    n = column.shape[0]
    return jnp.broadcast_to(column, (n, 128)).T[0:1, :]


def kernel(
    hid, w, tgt, cot, loss, gh, gw,
    hbuf, wbuf, pb, sx, rx, st, gall, gt, rb, zs, zr, fin, ys, yr, wst,
    lsem, hs, hr, xs, xr, ss, sr, gs, gr, ds_, dr, zss, zrs, yss, yrs, ws,
):
    x = lax.axis_index("dp")
    v = lax.axis_index("vocab")
    y, z, c = v // (2 * NZ), (v // 2) % NZ, v % 2
    oc = 1 - c

    def dev(dx=0, dy=0, dz=0, core=None):
        yy, zz = (y + dy) % NY, (z + dz) % NZ
        cc = c if core is None else core
        return {"dp": (x + dx) % NX, "vocab": (yy * NZ + zz) * 2 + cc}

    def remote(src, dst, send, recv, to):
        return pltpu.make_async_remote_copy(
            src_ref=src, dst_ref=dst, send_sem=send, recv_sem=recv,
            device_id=to, device_id_type=pl.DeviceIdType.MESH,
        )

    local = [pltpu.make_async_copy(w.at[pl.ds(h * 1024, 1024), :], wbuf.at[h], lsem.at[h]) for h in range(2)]
    for h in range(2):
        cols = pl.multiple_of(x * 2048 + h * 1024, 1024)
        local.append(pltpu.make_async_copy(hid.at[:, pl.ds(cols, 1024)], hbuf.at[h, 0], lsem.at[2 + h]))
    for d in local:
        d.start()

    barrier = pltpu.get_barrier_semaphore()
    peers = [dev(dx=k) for k in (1, 2, 3)] + [dev(core=oc)]
    peers += [dev(dy=k) for k in (1, 2, 3)] + [dev(dz=k) for k in range(1, NZ)]
    for p in peers:
        pl.semaphore_signal(barrier, inc=1, device_id=p, device_id_type=pl.DeviceIdType.MESH)
    pl.semaphore_wait(barrier, len(peers))

    order = (2, 1, 3)
    sent = []
    mine = pl.ds(pl.multiple_of(y * 64, 64), 64)
    take = {}
    for r in order:
        to = (4 - r) % 4
        cols = pl.multiple_of(((x + to) % NX) * 2048 + c * 1024, 1024)
        take[r] = remote(hid.at[mine, pl.ds(cols, 1024)], hbuf.at[c, r, mine, :], hs.at[r, 0], hr.at[r, 0], dev(dx=to))
        take[r].start()
        sent.append(take[r])
    around = {}
    for r in order:
        take[r].wait_recv()
        for k, dy in ((1, 1), (2, -1)):
            d = remote(hbuf.at[c, r, mine, :], hbuf.at[c, r, mine, :], hs.at[r, k], hr.at[r, k], dev(dy=dy))
            d.start()
            around[r, k] = d
            sent.append(d)

    for d in local:
        d.wait()

    def product(r):
        def step(n, carry):
            at = pl.ds(pl.multiple_of(n * 256, 256), 256)
            pb[r, :, at] = jnp.dot(hbuf[0, r], wbuf[0, :, at], preferred_element_type=F32) + jnp.dot(
                hbuf[1, r], wbuf[1, :, at], preferred_element_type=F32
            )
            return carry

        lax.fori_loop(0, 4, step, 0)

    product(0)

    def forward(r):
        around[r, 1].wait_recv()
        rows = pl.ds(pl.multiple_of(((y + 3) % NY) * 64, 64), 32)
        d = remote(hbuf.at[c, r, rows, :], hbuf.at[c, r, rows, :], hs.at[r, 3], hr.at[r, 3], dev(dy=1))
        d.start()
        around[r, 3] = d
        around[r, 2].wait_recv()
        rows = pl.ds(pl.multiple_of(((y + 1) % NY) * 64 + 32, 32), 32)
        e = remote(hbuf.at[c, r, rows, :], hbuf.at[c, r, rows, :], hs.at[r, 4], hr.at[r, 4], dev(dy=-1))
        e.start()
        around[r, 4] = e
        sent.extend((d, e))

    across = {}

    def share(r):
        around[r, 3].wait_recv()
        around[r, 4].wait_recv()
        d = remote(hbuf.at[c, r], hbuf.at[c, r], hs.at[r, 5], hr.at[r, 5], dev(core=oc))
        d.start()
        across[r] = d
        sent.append(d)

    RIGHT, LEFT = 1, -1
    ring = {}

    def send_x(k, dx):
        d = remote(sx.at[k], rx.at[k], xs.at[k], xr.at[k], dev(dx=dx))
        d.start()
        ring[k] = d
        sent.append(d)

    top, low = slice(0, 128), slice(128, 256)
    forward(2)
    forward(1)
    share(2)
    forward(3)
    share(1)
    across[2].wait_recv()
    product(2)
    pack_tall(pb[2, top, :], sx.at[0])
    send_x(0, RIGHT)
    pack_tall(pb[2, low, :], sx.at[1])
    send_x(1, LEFT)
    share(3)
    across[1].wait_recv()
    product(1)
    pack_tall(pb[1, low, :], sx.at[2])
    send_x(2, RIGHT)
    across[3].wait_recv()
    product(3)
    pack_tall(pb[3, top, :], sx.at[3])
    send_x(3, LEFT)
    ring[0].wait_recv()
    pack_tall(pb[1, top, :] + unpack_tall(rx.at[0], 128, 1024), sx.at[4])
    send_x(4, RIGHT)
    ring[1].wait_recv()
    pack_tall(pb[3, low, :] + unpack_tall(rx.at[1], 128, 1024), sx.at[5])
    send_x(5, LEFT)
    ring[2].wait_recv()
    pb[0, low, :] += unpack_tall(rx.at[2], 128, 1024)
    ring[3].wait_recv()
    pb[0, top, :] += unpack_tall(rx.at[3], 128, 1024)
    ring[4].wait_recv()
    pb[0, top, :] += unpack_tall(rx.at[4], 128, 1024)
    ring[5].wait_recv()
    pb[0, low, :] += unpack_tall(rx.at[5], 128, 1024)

    target = as_column(tgt[...].astype(F32))
    weigh = as_column(cot[...])
    first = (v * 1024).astype(F32)
    lanes = lax.broadcasted_iota(jnp.int32, (128, 1024), 1).astype(F32) + first
    tops, sums, picks = [], [], []
    for half in (top, low):
        logit = pb[0, half, :]
        m = jnp.max(logit, axis=1, keepdims=True)
        hot = lanes == target[half]
        picks.append(jnp.sum(jnp.where(hot, logit, 0.0), axis=1, keepdims=True))
        e = jnp.exp(logit - m)
        pb[0, half, :] = e
        tops.append(m)
        sums.append(jnp.sum(e, axis=1, keepdims=True))
    own_top = jnp.concatenate(tops, axis=0)
    st[0, 0, 0:1, :] = as_line(own_top)
    st[0, 0, 1:2, :] = as_line(jnp.concatenate(sums, axis=0))
    st[0, 0, 2:3, :] = as_line(jnp.concatenate(picks, axis=0))

    def join(level, places, out):
        for k, p in enumerate(places, 1):
            d = remote(st.at[level, 0], st.at[level, k], ss.at[level, k], sr.at[level, k], p)
            d.start()
            sent.append(d)
            places[k - 1] = d
        for d in places:
            d.wait_recv()
        n = len(places) + 1
        m = st[level, 0, 0:1, :]
        for k in range(1, n):
            m = jnp.maximum(m, st[level, k, 0:1, :])
        s = jnp.zeros_like(m)
        q = jnp.zeros_like(m)
        for k in range(n):
            s = s + st[level, k, 1:2, :] * jnp.exp(st[level, k, 0:1, :] - m)
            q = q + st[level, k, 2:3, :]
        st[out, 0, 0:1, :] = m
        st[out, 0, 1:2, :] = s
        st[out, 0, 2:3, :] = q
        return m, s, q

    join(0, [dev(core=oc)], 1)
    join(1, [dev(dz=k) for k in range(1, NZ)], 2)
    m, s, q = join(2, [dev(dy=k) for k in (1, 2, 3)], 3)
    loss[...] = m + jnp.log(s) - q
    all_top, all_sum = as_column(m), as_column(s)
    for i, half in enumerate((top, low)):
        factor = jnp.exp(own_top[half] - all_top[half]) / all_sum[half]
        hot = (lanes == target[half]).astype(F32)
        gall[0, half, :] = (weigh[half] * (pb[0, half, :] * factor - hot)).astype(BF16)

    def send_g(k, src, dst, half, dx):
        d = remote(gall.at[src, half, :], gall.at[dst, half, :], gs.at[k], gr.at[k], dev(dx=dx))
        d.start()
        sent.append(d)
        return d

    T, L = pl.ds(0, 128), pl.ds(128, 128)
    a0 = send_g(0, 0, 3, T, RIGHT)
    b0 = send_g(1, 0, 1, L, LEFT)
    a1 = send_g(2, 0, 3, L, RIGHT)
    b1 = send_g(3, 0, 1, T, LEFT)

    pair, zd = {}, {}

    def block_product(r):
        for h in range(2):
            def step(n, carry, h=h):
                at = pl.ds(pl.multiple_of(n * 256, 256), 256)
                out = pl.ds(pl.multiple_of(n * 256 + h * 1024, 256), 256)
                res = lax.dot_general(gall[r], wbuf[h, at, :], NEG, preferred_element_type=F32)
                gt[r, :, :, :, out] = res.reshape(NZ, 2, 16, 256)
                return carry

            lax.fori_loop(0, 4, step, 0)
        d = remote(gt.at[r, :, oc], rb.at[r], ds_.at[r], dr.at[r], dev(core=oc))
        d.start()
        pair[r] = d
        sent.append(d)

    def piece(r, k):
        zz = (z + k) % NZ
        return gt[r, zz, c] + rb[r, zz]

    def send_z(r, d, k, rows):
        cp = remote(
            zs.at[r, d, k, pl.ds(0, rows), :], zr.at[r, d, k, pl.ds(0, rows), :],
            zss.at[r, d, k], zrs.at[r, d, k], dev(dz=1 if d == 0 else -1),
        )
        cp.start()
        zd[r, d, k] = cp
        sent.append(cp)

    def z_step(r, k):
        if k == 0:
            pair[r].wait_recv()
            far = piece(r, 4)
            pack_flat(far[:, :1024], zs.at[r, 0, 0])
            send_z(r, 0, 0, 144)
            pack_flat(far[:, 1024:], zs.at[r, 1, 0])
            send_z(r, 1, 0, 144)
        elif k < 4:
            for d in range(2):
                val = piece(r, 4 - k if d == 0 else 4 + k)
                zd[r, d, k - 1].wait_recv()
                got = zr.at[r, d, k - 1]
                if k == 1:
                    part = unpack_flat(got, 16, 1024)
                    none = jnp.zeros_like(part)
                    val = val + jnp.concatenate([part, none] if d == 0 else [none, part], axis=1)
                else:
                    val = val + unpack_flat(got, 16, 2048)
                pack_flat(val, zs.at[r, d, k])
                send_z(r, d, k, 272)
        else:
            val = piece(r, 0)
            for d in range(2):
                zd[r, d, 3].wait_recv()
                val = val + unpack_flat(zr.at[r, d, 3], 16, 2048)
            fin[r] = val

    def weight_tile(f):
        h, at = f // 4, pl.ds((f % 4) * 256, 256)
        lhs = hbuf[h, :, :, at].reshape(1024, 256)
        rhs = gall[...].reshape(1024, 1024)
        out = lax.dot_general(lhs, rhs, (((0,), (0,)), ((), ())), preferred_element_type=F32)
        wst[f] = out.astype(BF16)
        d = pltpu.make_async_copy(wst.at[f], gw.at[pl.ds(f * 256, 256), :], ws.at[f])
        d.start()
        return d

    block_product(0)
    a0.wait_recv()
    f0 = send_g(4, 3, 2, T, RIGHT)
    b0.wait_recv()
    f1 = send_g(5, 1, 2, L, LEFT)
    z_step(0, 0)
    z_step(0, 1)
    a1.wait_recv()
    block_product(3)
    z_step(0, 2)
    b1.wait_recv()
    block_product(1)
    z_step(3, 0)
    z_step(0, 3)
    z_step(1, 0)
    z_step(3, 1)
    z_step(0, 4)
    f0.wait_recv()
    f1.wait_recv()
    block_product(2)
    z_step(1, 1)
    z_step(3, 2)
    z_step(2, 0)
    tiles = [weight_tile(0)]
    z_step(1, 2)
    z_step(3, 3)
    tiles.append(weight_tile(1))
    z_step(2, 1)
    z_step(3, 4)
    z_step(1, 3)
    tiles.append(weight_tile(2))
    z_step(2, 2)
    z_step(1, 4)
    tiles.append(weight_tile(3))
    tiles.append(weight_tile(4))
    z_step(2, 3)
    tiles.append(weight_tile(5))
    z_step(2, 4)

    def held(k):
        return fin[(y + k - x + NX) % NX]

    def send_y(k, rows, dy):
        d = remote(ys.at[k, pl.ds(0, rows), :], yr.at[k, pl.ds(0, rows), :], yss.at[k], yrs.at[k], dev(dy=dy))
        d.start()
        sent.append(d)
        return d

    far = held(2)
    pack_flat(far[:, :1024], ys.at[0])
    y0 = send_y(0, 144, 1)
    pack_flat(far[:, 1024:], ys.at[1])
    y1 = send_y(1, 144, -1)
    tiles.append(weight_tile(6))
    none = jnp.zeros((16, 1024), F32)
    y0.wait_recv()
    pack_flat(held(1) + jnp.concatenate([unpack_flat(yr.at[0], 16, 1024), none], axis=1), ys.at[2])
    y2 = send_y(2, 272, 1)
    y1.wait_recv()
    pack_flat(held(3) + jnp.concatenate([none, unpack_flat(yr.at[1], 16, 1024)], axis=1), ys.at[3])
    y3 = send_y(3, 272, -1)
    tiles.append(weight_tile(7))
    y2.wait_recv()
    y3.wait_recv()
    gh[...] = (held(0) + unpack_flat(yr.at[2], 16, 2048) + unpack_flat(yr.at[3], 16, 2048)).astype(BF16)

    for d in sent:
        d.wait_send()
    for d in tiles:
        d.wait()


def shards(hidden, weight, targets, cotangent):
    vm, dma = pltpu.VMEM, pltpu.SemaphoreType.DMA
    space = pl.BlockSpec(memory_space=pltpu.VMEM)
    raw = pl.BlockSpec(memory_space=pl.ANY)
    loss, gh, gw = pl.pallas_call(
        kernel,
        out_shape=(
            jax.ShapeDtypeStruct((1, 256), F32),
            jax.ShapeDtypeStruct((16, 2048), BF16),
            jax.ShapeDtypeStruct((2048, 1024), BF16),
        ),
        in_specs=[raw, raw, space, space],
        out_specs=(space, space, raw),
        scratch_shapes=[
            vm((2, 4, 256, 1024), BF16),
            vm((2, 1024, 1024), BF16),
            vm((4, 256, 1024), F32),
            vm((6, 1040, 128), I16),
            vm((6, 1040, 128), I16),
            vm((4, 8, 8, 256), F32),
            vm((4, 256, 1024), BF16),
            vm((4, NZ, 2, 16, 2048), F32),
            vm((4, NZ, 16, 2048), F32),
            vm((4, 2, 4, 272, 128), I16),
            vm((4, 2, 4, 272, 128), I16),
            vm((4, 16, 2048), F32),
            vm((4, 272, 128), I16),
            vm((4, 272, 128), I16),
            vm((8, 256, 1024), BF16),
            dma((4,)), dma((4, 6)), dma((4, 6)), dma((6,)), dma((6,)),
            dma((3, 8)), dma((3, 8)), dma((6,)), dma((6,)), dma((4,)), dma((4,)),
            dma((4, 2, 4)), dma((4, 2, 4)), dma((4,)), dma((4,)), dma((8,)),
        ],
        compiler_params=pltpu.CompilerParams(
            collective_id=0, has_side_effects=True, vmem_limit_bytes=60 * 1024 * 1024
        ),
    )(hidden, weight, targets.reshape(1, 256), cotangent.reshape(1, 256))
    return loss.reshape(256), gh, gw


def solution(mesh):
    in_specs = (P("dp", None), P("dp", "vocab"), P("dp"), P("dp"))
    out_specs = (P("dp"), P("vocab", "dp"), P("dp", "vocab"))
    return jax.shard_map(shards, mesh=mesh, in_specs=in_specs, out_specs=out_specs, check_vma=False)
```

time: 358 us -> 127 us (0.35); the launches traced: 353 us -> 127 us
  waiting for transfers between devices: 181 us -> 0 us
  Pallas kernels: 0 us -> 119 us
  blocking collectives: 102 us -> 0 us
  matrix products: 24.8 us -> 0 us
  local copies, waits for them, and re-layouts: 24.5 us -> 7.34 us
  between operations: 14.2 us -> 0.64 us
  other arithmetic: 5.72 us -> 0 us
    reduce_scatter x2 -> x0, waiting for transfers between devices: 181 us -> none  [the longest x1 128 us: shards(): lax.psum_scatter(lax.dot_general(row_block, weight, (((1,), (1,)), ((), (...]
    pallas_call x0 -> x1, Pallas kernels: none -> 119 us  [shards(): pl.pallas_call(kernel, out_shape=(jax.ShapeDtypeStruct((1, 256), F32), ja...]
    all_to_all x3 -> x0, blocking collectives: 102 us -> none  [the longest x1 51.6 us: shards(): lax.all_to_all(hidden, 'dp', split_axis=1, concat_axis=0, tiled=True)]
    dot_general x3 -> x0, matrix products: 24.8 us -> none  [the longest x1 10.6 us: shards(): lax.dot_general(row_block, weight, (((1,), (1,)), ((), ())), preferred_el...]
    all_to_all x2 -> x0, local copies, waits for them, and re-layouts: 8.63 us -> none  [the longest x1 6.27 us: shards(): lax.all_to_all(hidden, 'dp', split_axis=1, concat_axis=0, tiled=True)]
    unnamed x13 -> x3, local copies, waits for them, and re-layouts: 14.8 us -> 7.34 us
  transfers between devices with their start and end apart: 2 -> 0, of which waited for: 2 -> 0; matrix products, arithmetic and copies ran while one was open for 4% -> 0% of each run, Pallas kernels for 0% -> 0%
where the time goes in v1:
time: 127 us
  Pallas kernels  119 us (94%)
  local copies, waits for them, and re-layouts  7.34 us (6%)
    pallas_call x1, Pallas kernels, shards(): pl.pallas_call(kernel, out_shape=(jax.ShapeDtypeStruct((1, 256), F32), ja...  119 us
    unnamed x3, local copies, waits for them, and re-layouts  7.34 us

profile of v1, /device:TPU:1, one launch (start us, length us, event | category | flops | bytes accessed | tf_op | source)
XLA Modules:
  0.0 126.6 jit_solution(8278745484544788077)
XLA Ops:
  0.6 118.6 %shard_map.67 = (f32[1,256]{1,0:T(1,128)}, bf16[16,2048]{1,0:T(8,128)(2,1)}, bf16[2048,1024]{1,0:T(8,128)(2,1)}) custom-call(bf16[256,8192]{1,0:T(8,128)(2,1)} %hid.1, bf16[2048,1024]{1,0:T(8,128)(2,1)} %w.1, s32[1,256]{1,0:T(1,128)} %bitcast.3, f32[1,256]{1,0:T(1,128)} %bitcast.4), custom_call_target="tpu_custom_call" | custom-call | tf_op jit(solution)/shard_map/pallas_call | solution.py:411
  119.3 1.2 copy.10
  120.5 1.5 %copy.11 = bf16[16,2048]{1,0:T(8,128)(2,1)} copy(bf16[16,2048]{1,0:T(8,128)(2,1)} %get-tuple-element.13) | data formatting | bytes 131072
  122.0 4.6 %copy.12 = bf16[2048,1024]{1,0:T(8,128)(2,1)} copy(bf16[2048,1024]{1,0:T(8,128)(2,1)} %get-tuple-element.14) | data formatting | bytes 8388608

commit v2 on v1

v2 whole, which is shorter than its diff:
```python
import jax
import jax.numpy as jnp
from jax import lax
from jax.experimental import pallas as pl
from jax.experimental.pallas import tpu as pltpu
from jax.sharding import PartitionSpec as P

F32, BF16, I16 = jnp.float32, jnp.bfloat16, jnp.int16
NX, NY, NZ = 4, 4, 8
FINE = 64.0 / 0.6931471805599453
TOP = 32700.0


def row_code(x):
    top = jnp.max(jnp.abs(x), axis=1, keepdims=True)
    return jnp.ceil(jnp.log(jnp.maximum(top, 1e-30)) * FINE)


def pack_tall(x, dst):
    rows, cols = x.shape
    k = row_code(x)
    inv = jnp.exp(k * (-1.0 / FINE)) * TOP
    for j in range(cols // 128):
        dst[j * rows : (j + 1) * rows, :] = jnp.round(x[:, j * 128 : (j + 1) * 128] * inv).astype(I16)
    line = jnp.broadcast_to(k, (rows, 128)).T[0:1, :]
    dst[cols // 128 * rows : cols // 128 * rows + 16, :] = jnp.broadcast_to(line, (16, 128)).astype(I16)


def unpack_tall(src, rows, cols):
    at = cols // 128 * rows
    line = src[at : at + 16, :].astype(F32)[0:1, :]
    k = jnp.broadcast_to(line, (rows, rows)).T
    scale = jnp.exp(k * (1.0 / FINE)) * (1.0 / TOP)
    return jnp.concatenate(
        [src[j * rows : (j + 1) * rows, :].astype(F32) * scale for j in range(cols // 128)], axis=1
    )


def pack_flat(x, dst):
    rows, cols = x.shape
    k = row_code(x)
    inv = jnp.exp(k * (-1.0 / FINE)) * TOP
    for j in range(cols // 128):
        dst[j * rows : (j + 1) * rows, :] = jnp.round(x[:, j * 128 : (j + 1) * 128] * inv).astype(I16)
    dst[cols // 128 * rows : (cols // 128 + 1) * rows, :] = jnp.broadcast_to(k, (rows, 128)).astype(I16)


def unpack_flat(src, rows, cols):
    at = cols // 128 * rows
    scale = jnp.exp(src[at : at + rows, :].astype(F32) * (1.0 / FINE)) * (1.0 / TOP)
    return jnp.concatenate(
        [src[j * rows : (j + 1) * rows, :].astype(F32) * scale for j in range(cols // 128)], axis=1
    )


def as_column(line):
    n = line.shape[1]
    return jnp.broadcast_to(line, (128, n)).T[:, 0:1]


def as_line(column):
    n = column.shape[0]
    return jnp.broadcast_to(column, (n, 128)).T[0:1, :]


def kernel(
    hid, w, tgt_in, cot_in, loss, gh, gw,
    tgt, cot,    hbuf, wbuf, wt, pb, sx, rx, st, eb, fx, gall, gt, rb, zs, zr, fin, ys, yr,
    lsem, hs, hr, xs, xr, ss, sr, gs, gr, fs, fr, ds_, dr, zss, zrs, yss, yrs,
):
    x = lax.axis_index("dp")
    v = lax.axis_index("vocab")
    y, z, c = v // (2 * NZ), (v // 2) % NZ, v % 2
    oc = 1 - c

    def dev(dx=0, dy=0, dz=0, core=None):
        yy, zz = (y + dy) % NY, (z + dz) % NZ
        cc = c if core is None else core
        return {"dp": (x + dx) % NX, "vocab": (yy * NZ + zz) * 2 + cc}

    def remote(src, dst, send, recv, to):
        return pltpu.make_async_remote_copy(
            src_ref=src, dst_ref=dst, send_sem=send, recv_sem=recv,
            device_id=to, device_id_type=pl.DeviceIdType.MESH,
        )

    local = [pltpu.make_async_copy(w.at[pl.ds(h * 1024, 1024), :], wbuf.at[h], lsem.at[h]) for h in range(2)]
    for h in range(2):
        cols = pl.multiple_of(x * 2048 + h * 1024, 1024)
        local.append(pltpu.make_async_copy(hid.at[:, pl.ds(cols, 1024)], hbuf.at[h, 0], lsem.at[2 + h]))
    local.append(pltpu.make_async_copy(tgt_in, tgt, lsem.at[4]))
    local.append(pltpu.make_async_copy(cot_in, cot, lsem.at[5]))
    for d in local:
        d.start()

    barrier = pltpu.get_barrier_semaphore()
    peers = [dev(dx=k) for k in (1, 2, 3)] + [dev(core=oc)]
    peers += [dev(dy=k) for k in (1, 2, 3)] + [dev(dz=k) for k in range(1, NZ)]
    for p in peers:
        pl.semaphore_signal(barrier, inc=1, device_id=p, device_id_type=pl.DeviceIdType.MESH)
    pl.semaphore_wait(barrier, len(peers))

    sent = []
    mine = pl.ds(pl.multiple_of(y * 64, 64), 64)
    take = {}
    def columns_for(r):
        to = (4 - r) % 4
        return to, pl.ds(pl.multiple_of(((x + to) % NX) * 2048 + c * 1024, 1024), 1024)

    to, cols = columns_for(2)
    take[2] = remote(hid.at[mine, cols], hbuf.at[c, 2, mine, :], hs.at[2, 0], hr.at[2, 0], dev(dx=to))
    take[2].start()
    sent.append(take[2])

    def direct(r):
        to, cols = columns_for(r)
        take[r] = remote(hid.at[:, cols], hbuf.at[c, r], hs.at[r, 0], hr.at[r, 0], dev(dx=to))
        take[r].start()
        sent.append(take[r])

    around = {}

    def along_y(k, rows, dy):
        d = remote(hbuf.at[c, 2, rows, :], hbuf.at[c, 2, rows, :], hs.at[2, k], hr.at[2, k], dev(dy=dy))
        d.start()
        around[k] = d
        sent.append(d)

    def rows_of(dy, half):
        return pl.ds(pl.multiple_of(((y + dy) % NY) * 64 + half * 32, 32), 32)

    def spread():
        take[2].wait_recv()
        along_y(1, rows_of(0, 0), 1)
        along_y(2, rows_of(0, 1), -1)
        along_y(3, rows_of(0, 1), 1)
        along_y(4, rows_of(0, 0), -1)

    def forward():
        around[1].wait_recv()
        along_y(5, rows_of(-1, 0), 1)
        around[2].wait_recv()
        along_y(6, rows_of(1, 1), -1)

    across = {}

    def share(r):
        if r == 2:
            for k in (3, 4, 5, 6):
                around[k].wait_recv()
        else:
            take[r].wait_recv()
        d = remote(hbuf.at[c, r], hbuf.at[c, r], hs.at[r, 7], hr.at[r, 7], dev(core=oc))
        d.start()
        across[r] = d
        sent.append(d)

    def product(r, core, add):
        def step(n, carry):
            at = pl.ds(pl.multiple_of(n * 256, 256), 256)
            res = jnp.dot(hbuf[core, r], wbuf[core, :, at], preferred_element_type=F32)
            pb[r, :, at] = pb[r, :, at] + res if add else res
            return carry

        lax.fori_loop(0, 4, step, 0)

    def arrived(r):
        across[r].wait_recv()

    RIGHT, LEFT = 1, -1
    ring = {}

    def send_x(k, dx):
        d = remote(sx.at[k], rx.at[k], xs.at[k], xr.at[k], dev(dx=dx))
        d.start()
        ring[k] = d
        sent.append(d)

    top, low = slice(0, 128), slice(128, 256)
    spread()
    direct(1)
    direct(3)
    for d in local:
        d.wait()
    product(0, 0, False)
    forward()
    product(0, 1, True)
    share(2)
    product(2, c, False)
    arrived(2)
    product(2, oc, True)
    pack_tall(pb[2, top, :], sx.at[0])
    send_x(0, RIGHT)
    pack_tall(pb[2, low, :], sx.at[1])
    send_x(1, LEFT)
    share(1)
    share(3)
    product(1, c, False)
    arrived(1)
    product(1, oc, True)
    pack_tall(pb[1, low, :], sx.at[2])
    send_x(2, RIGHT)
    product(3, c, False)
    arrived(3)
    product(3, oc, True)
    pack_tall(pb[3, top, :], sx.at[3])
    send_x(3, LEFT)
    ring[0].wait_recv()
    pack_tall(pb[1, top, :] + unpack_tall(rx.at[0], 128, 1024), sx.at[4])
    send_x(4, RIGHT)
    ring[1].wait_recv()
    pack_tall(pb[3, low, :] + unpack_tall(rx.at[1], 128, 1024), sx.at[5])
    send_x(5, LEFT)
    ring[2].wait_recv()
    pb[0, low, :] += unpack_tall(rx.at[2], 128, 1024)
    ring[3].wait_recv()
    pb[0, top, :] += unpack_tall(rx.at[3], 128, 1024)
    ring[4].wait_recv()
    pb[0, top, :] += unpack_tall(rx.at[4], 128, 1024)
    ring[5].wait_recv()
    pb[0, low, :] += unpack_tall(rx.at[5], 128, 1024)

    target = as_column(tgt[...].astype(F32))
    first = (v * 1024).astype(F32)
    lanes = lax.broadcasted_iota(jnp.int32, (128, 1024), 1).astype(F32) + first

    def send_e(k, src, dst, half, dx):
        d = remote(eb.at[src, half, :], eb.at[dst, half, :], gs.at[k], gr.at[k], dev(dx=dx))
        d.start()
        sent.append(d)
        return d

    upper, lower = pl.ds(0, 128), pl.ds(128, 128)
    tops, sums, picks = [], [], []
    for half in (top, low):
        logit = pb[0, half, :]
        m = jnp.max(logit, axis=1, keepdims=True)
        hot = lanes == target[half]
        picks.append(jnp.sum(jnp.where(hot, logit, 0.0), axis=1, keepdims=True))
        e = jnp.exp(logit - m)
        eb[0, half, :] = e.astype(BF16)
        pb[0, half, :] = e
        tops.append(m)
        sums.append(jnp.sum(e, axis=1, keepdims=True))
    a0 = send_e(0, 0, 3, upper, RIGHT)
    b0 = send_e(1, 0, 1, lower, LEFT)
    a1 = send_e(2, 0, 3, lower, RIGHT)
    b1 = send_e(3, 0, 1, upper, LEFT)
    st[0, 0, 0:1, :] = as_line(jnp.concatenate(tops, axis=0))
    st[0, 0, 1:2, :] = as_line(jnp.concatenate(sums, axis=0))
    st[0, 0, 2:3, :] = as_line(jnp.concatenate(picks, axis=0))

    def tell(level, places):
        out = []
        for k, p in enumerate(places, 1):
            d = remote(st.at[level, 0], st.at[level, k], ss.at[level, k], sr.at[level, k], p)
            d.start()
            sent.append(d)
            out.append(d)
        return out

    def join(level, told, out):
        for d in told:
            d.wait_recv()
        n = len(told) + 1
        m = st[level, 0, 0:1, :]
        for k in range(1, n):
            m = jnp.maximum(m, st[level, k, 0:1, :])
        s = jnp.zeros_like(m)
        q = jnp.zeros_like(m)
        for k in range(n):
            s = s + st[level, k, 1:2, :] * jnp.exp(st[level, k, 0:1, :] - m)
            q = q + st[level, k, 2:3, :]
        st[out, 0, 0:1, :] = m
        st[out, 0, 1:2, :] = s
        st[out, 0, 2:3, :] = q
        return m, s, q

    def turn(h):
        def step(n, carry):
            at = pl.ds(pl.multiple_of(n * 256, 256), 256)
            wt[h, :, at] = wbuf[h, at, :].T
            return carry

        lax.fori_loop(0, 4, step, 0)

    told = tell(0, [dev(core=oc)])
    join(0, told, 1)
    told = tell(1, [dev(dz=k) for k in range(1, NZ)])
    turn(0)
    join(1, told, 2)
    told = tell(2, [dev(dy=k) for k in (1, 2, 3)])
    turn(1)
    m, s, q = join(2, told, 3)
    loss[...] = m + jnp.log(s) - q
    weigh = cot[...]
    fx[0, 0:1, :] = weigh * (jnp.exp(st[0, 0, 0:1, :] - m) / s)
    fx[0, 1:2, :] = weigh * (jnp.exp(q - m) / s - 1.0)
    fx[0, 2:3, :] = tgt[...].astype(F32)
    line = {}
    for k in (1, 3, 2):
        r = 4 - k
        line[r] = remote(fx.at[0], fx.at[r], fs.at[r], fr.at[r], dev(dx=k))
        line[r].start()
        sent.append(line[r])

    def scale(r):
        if r:
            line[r].wait_recv()
        factor, at_target, target = (as_column(fx[r, i : i + 1, :]) for i in range(3))
        for half in (top, low):
            e = eb[r, half, :].astype(F32) if r else pb[0, half, :]
            g = jnp.where(lanes == target[half], at_target[half], e * factor[half])
            gall[r, half, :] = g.astype(BF16)

    pair, zd = {}, {}

    def block_product(*blocks):
        def step(n, carry):
            at = pl.ds(pl.multiple_of((n % 4) * 256, 256), 256)
            out = pl.ds(pl.multiple_of(n * 256, 256), 256)
            lhs = jnp.concatenate([gall[r] for r in blocks], axis=0)
            res = jnp.dot(lhs, wt[n // 4, :, at], preferred_element_type=F32)
            for i, r in enumerate(blocks):
                gt[r, :, :, :, out] = res[i * 256 : (i + 1) * 256].reshape(NZ, 2, 16, 256)
            return carry

        lax.fori_loop(0, 8, step, 0)
        for r in blocks:
            d = remote(gt.at[r, :, oc], rb.at[r], ds_.at[r], dr.at[r], dev(core=oc))
            d.start()
            pair[r] = d
            sent.append(d)

    def z_half(r, k, d, half):
        zz = (z + (4 - k if d == 0 else 4 + k)) % NZ
        cols = pl.ds(half * 1024, 1024)
        val = gt[r, zz, c, :, cols] + rb[r, zz, :, cols]
        if k > 1 or (k == 1 and half == d):
            zd[r, d, k - 1, half].wait_recv()
            val = val + unpack_flat(zr.at[r, d, k - 1, half], 16, 1024)
        if k == 4:
            return val
        pack_flat(val, zs.at[r, d, k, half])
        cp = remote(
            zs.at[r, d, k, half], zr.at[r, d, k, half],
            zss.at[r, d, k, half], zrs.at[r, d, k, half], dev(dz=1 if d == 0 else -1),
        )
        cp.start()
        zd[r, d, k, half] = cp
        sent.append(cp)

    def z_step(r, k):
        if k == 0:
            pair[r].wait_recv()
        if k < 4:
            for d in range(2):
                z_half(r, k, d, d)
        if k < 3:
            for d in range(2):
                z_half(r, k + 1, d, 1 - d)
        if k == 4:
            for half in (0, 1):
                other = zd[r, 1, 3, half]
                val = z_half(r, 4, 0, half)
                other.wait_recv()
                fin[r, :, half * 1024 : half * 1024 + 1024] = val + unpack_flat(zr.at[r, 1, 3, half], 16, 1024)

    def weight_tile(f):
        h, at = f // 4, pl.ds((f % 4) * 256, 256)
        lhs = hbuf[h, :, :, at].reshape(1024, 256)
        rhs = gall[...].reshape(1024, 1024)
        out = lax.dot_general(lhs, rhs, (((0,), (0,)), ((), ())), preferred_element_type=F32)
        gw[f * 256 : (f + 1) * 256, :] = out.astype(BF16)

    a0.wait_recv()
    f0 = send_e(4, 3, 2, upper, RIGHT)
    b0.wait_recv()
    f1 = send_e(5, 1, 2, lower, LEFT)
    scale(0)
    block_product(0)
    z_step(0, 0)
    a1.wait_recv()
    scale(3)
    b1.wait_recv()
    scale(1)
    block_product(3, 1)
    z_step(0, 1)
    f0.wait_recv()
    f1.wait_recv()
    scale(2)
    z_step(3, 0)
    block_product(2)
    z_step(1, 0)
    z_step(0, 2)
    z_step(2, 0)
    z_step(3, 1)
    z_step(1, 1)
    z_step(0, 3)
    z_step(2, 1)
    z_step(3, 2)
    z_step(1, 2)
    z_step(0, 4)
    z_step(2, 2)
    z_step(3, 3)
    z_step(1, 3)
    weight_tile(0)
    z_step(2, 3)
    z_step(3, 4)
    weight_tile(1)
    z_step(1, 4)
    weight_tile(2)
    weight_tile(3)
    z_step(2, 4)

    def held(k):
        return fin[(y + k - x + NX) % NX]

    home = []
    for k in (2, 1, 3):
        pack_flat(held(k), ys.at[k])
        d = remote(ys.at[k], yr.at[k], yss.at[k], yrs.at[k], dev(dy=k))
        d.start()
        sent.append(d)
        home.append((k, d))
    weight_tile(4)
    weight_tile(5)
    weight_tile(6)
    weight_tile(7)
    total = held(0)
    for k, d in home:
        d.wait_recv()
        total = total + unpack_flat(yr.at[k], 16, 2048)
    gh[...] = total.astype(BF16)

    def drain():
        for d in sent:
            d.wait_send()

    drain()


def finish(loss_in, gh_in, gw_in, loss, gh, gw, sem):
    pairs = ((gw_in, gw), (gh_in, gh), (loss_in, loss))
    copies = [pltpu.make_async_copy(a, b, sem.at[k]) for k, (a, b) in enumerate(pairs)]
    for d in copies:
        d.start()
    for d in copies:
        d.wait()


def shards(hidden, weight, targets, cotangent):
    vm, dma = pltpu.VMEM, pltpu.SemaphoreType.DMA
    space = pl.BlockSpec(memory_space=pltpu.VMEM)
    raw = pl.BlockSpec(memory_space=pl.ANY)
    loss, gh, gw = pl.pallas_call(
        kernel,
        out_shape=(
            jax.ShapeDtypeStruct((1, 256), F32),
            jax.ShapeDtypeStruct((16, 2048), BF16),
            jax.ShapeDtypeStruct((2048, 1024), BF16),
        ),
        in_specs=[pl.BlockSpec(memory_space=pltpu.HBM)] * 4,
        out_specs=(space, space, space),
        scratch_shapes=[
            vm((1, 256), jnp.int32),
            vm((1, 256), F32),
            vm((2, 4, 256, 1024), BF16),
            vm((2, 1024, 1024), BF16),
            vm((2, 1024, 1024), BF16),
            vm((4, 256, 1024), F32),
            vm((6, 1040, 128), I16),
            vm((6, 1040, 128), I16),
            vm((4, 8, 8, 256), F32),
            vm((4, 256, 1024), BF16),
            vm((4, 8, 256), F32),
            vm((4, 256, 1024), BF16),
            vm((4, NZ, 2, 16, 2048), F32),
            vm((4, NZ, 16, 2048), F32),
            vm((4, 2, 4, 2, 144, 128), I16),
            vm((4, 2, 4, 2, 144, 128), I16),
            vm((4, 16, 2048), F32),
            vm((4, 272, 128), I16),
            vm((4, 272, 128), I16),
            dma((6,)), dma((4, 8)), dma((4, 8)), dma((6,)), dma((6,)),
            dma((3, 8)), dma((3, 8)), dma((6,)), dma((6,)), dma((4,)), dma((4,)), dma((4,)), dma((4,)),
            dma((4, 2, 4, 2)), dma((4, 2, 4, 2)), dma((4,)), dma((4,)),
        ],
        compiler_params=pltpu.CompilerParams(
            collective_id=0, has_side_effects=True, vmem_limit_bytes=46 * 1024 * 1024
        ),
    )(hidden, weight, targets.reshape(1, 256), cotangent.reshape(1, 256))
    loss, gh, gw = pl.pallas_call(
        finish,
        out_shape=(
            jax.ShapeDtypeStruct((1, 256), F32),
            jax.ShapeDtypeStruct((16, 2048), BF16),
            jax.ShapeDtypeStruct((2048, 1024), BF16),
        ),
        in_specs=[space, space, space],
        out_specs=(raw, raw, raw),
        scratch_shapes=[dma((3,))],
        compiler_params=pltpu.CompilerParams(vmem_limit_bytes=8 * 1024 * 1024),
    )(loss, gh, gw)
    return loss.reshape(256), gh, gw


def solution(mesh):
    in_specs = (P("dp", None), P("dp", "vocab"), P("dp"), P("dp"))
    out_specs = (P("dp"), P("vocab", "dp"), P("dp", "vocab"))
    return jax.shard_map(shards, mesh=mesh, in_specs=in_specs, out_specs=out_specs, check_vma=False)
```

time: 127 us -> 106 us (0.83)
  Pallas kernels: 119 us -> 104 us
  local copies, waits for them, and re-layouts: 7.34 us -> 1.35 us
    pallas_call x1, Pallas kernels: 119 us -> 102 us  [shards(): pl.pallas_call(kernel, out_shape=(jax.ShapeDtypeStruct((1, 256), F32), ja...]
    unnamed x3 -> x4, local copies, waits for them, and re-layouts: 7.34 us -> 1.35 us
    pallas_call x0 -> x1, Pallas kernels: none -> 2.04 us  [shards(): pl.pallas_call(finish, out_shape=(jax.ShapeDtypeStruct((1, 256), F32), ja...]
where the time goes in v2:
time: 106 us
  Pallas kernels  104 us (98%)
  local copies, waits for them, and re-layouts  1.35 us (1%)
    pallas_call x1, Pallas kernels, shards(): pl.pallas_call(kernel, out_shape=(jax.ShapeDtypeStruct((1, 256), F32), ja...  102 us

profile of v2, /device:TPU:1, one launch (start us, length us, event | category | flops | bytes accessed | tf_op | source)
XLA Modules:
  0.0 105.8 jit_solution(8375954636385365966)
XLA Ops:
  0.6 0.0 copy-start
  0.6 0.7 copy-done
  1.3 0.0 copy-start.1
  1.3 0.7 copy-done.1
  2.0 101.6 %shard_map.67 = (f32[1,256]{1,0:T(1,128)S(1)}, bf16[16,2048]{1,0:T(8,128)(2,1)S(1)}, bf16[2048,1024]{1,0:T(8,128)(2,1)S(1)}) custom-call(bf16[256,8192]{1,0:T(8,128)(2,1)} %hid.1, bf16[2048,1024]{1,0:T(8,128)(2,1)} %w.1, s32[1,256]{1,0:T(1,128)S(1)} %bitcast.3, f32[1,256]{1,0:T(1,128)S(1)} %bitcast.4), custom_call_target="tpu_custom_call" | custom-call | tf_op jit(solution)/shard_map/pallas_call | solution.py:456
  103.6 2.0 %shard_map.68 = (f32[1,256]{1,0:T(1,128)}, bf16[16,2048]{1,0:T(8,128)(2,1)}, bf16[2048,1024]{1,0:T(8,128)(2,1)}) custom-call(f32[1,256]{1,0:T(1,128)S(1)} %get-tuple-element.9.loss_in, bf16[16,2048]{1,0:T(8,128)(2,1)S(1)} %get-tuple-element.10.gh_in, bf16[2048,1024]{1,0:T(8,128)(2,1)S(1)} %get-tuple-element.11.gw_in), custom_call_target="tpu_custom_call" | custom-call | tf_op jit(solution)/shard_map/pallas_call | solution.py:493
Async XLA Ops:
  0.6 0.7 copy-start
  1.3 0.7 copy-start.1

commit v3 on v2

--- a/solution.py
+++ b/solution.py
@@ -65,7 +65,7 @@
 
 def kernel(
     hid, w, tgt_in, cot_in, loss, gh, gw,
-    tgt, cot,    hbuf, wbuf, wt, pb, sx, rx, st, eb, fx, gall, gt, rb, zs, zr, fin, ys, yr,
+    tgt, cot,    hbuf, wbuf, wt, pb, sx, rx, st, eb, fx, gall, hot0, vt, gt, rb, zs, zr, fin, ys, yr,
     lsem, hs, hr, xs, xr, ss, sr, gs, gr, fs, fr, ds_, dr, zss, zrs, yss, yrs,
 ):
     x = lax.axis_index("dp")
@@ -95,7 +95,7 @@
 
     barrier = pltpu.get_barrier_semaphore()
     peers = [dev(dx=k) for k in (1, 2, 3)] + [dev(core=oc)]
-    peers += [dev(dy=k) for k in (1, 2, 3)] + [dev(dz=k) for k in range(1, NZ)]
+    peers += [dev(dy=k, core=cc) for k in (1, 2, 3) for cc in (c, oc)] + [dev(dz=k) for k in range(1, NZ)]
     for p in peers:
         pl.semaphore_signal(barrier, inc=1, device_id=p, device_id_type=pl.DeviceIdType.MESH)
     pl.semaphore_wait(barrier, len(peers))
@@ -108,20 +108,20 @@
         return to, pl.ds(pl.multiple_of(((x + to) % NX) * 2048 + c * 1024, 1024), 1024)
 
     to, cols = columns_for(2)
-    take[2] = remote(hid.at[mine, cols], hbuf.at[c, 2, mine, :], hs.at[2, 0], hr.at[2, 0], dev(dx=to))
+    take[2] = remote(hid.at[mine, cols], hbuf.at[c, 2, mine, :], hs.at[0], hr.at[0], dev(dx=to))
     take[2].start()
     sent.append(take[2])
 
     def direct(r):
         to, cols = columns_for(r)
-        take[r] = remote(hid.at[:, cols], hbuf.at[c, r], hs.at[r, 0], hr.at[r, 0], dev(dx=to))
+        take[r] = remote(hid.at[:, cols], hbuf.at[c, r], hs.at[r], hr.at[r], dev(dx=to))
         take[r].start()
         sent.append(take[r])
 
     around = {}
 
     def along_y(k, rows, dy):
-        d = remote(hbuf.at[c, 2, rows, :], hbuf.at[c, 2, rows, :], hs.at[2, k], hr.at[2, k], dev(dy=dy))
+        d = remote(hbuf.at[c, 2, rows, :], hbuf.at[c, 2, rows, :], hs.at[3 + k], hr.at[3 + k], dev(dy=dy))
         d.start()
         around[k] = d
         sent.append(d)
@@ -150,7 +150,7 @@
                 around[k].wait_recv()
         else:
             take[r].wait_recv()
-        d = remote(hbuf.at[c, r], hbuf.at[c, r], hs.at[r, 7], hr.at[r, 7], dev(core=oc))
+        d = remote(hbuf.at[c, r], hbuf.at[c, r], hs.at[9 + r], hr.at[9 + r], dev(core=oc))
         d.start()
         across[r] = d
         sent.append(d)
@@ -166,6 +166,14 @@
 
     def arrived(r):
         across[r].wait_recv()
+
+    def turn(h):
+        def step(n, carry):
+            at = pl.ds(pl.multiple_of(n * 256, 256), 256)
+            wt[h, :, at] = wbuf[h, at, :].T
+            return carry
+
+        lax.fori_loop(0, 4, step, 0)
 
     RIGHT, LEFT = 1, -1
     ring = {}
@@ -211,6 +219,8 @@
     ring[1].wait_recv()
     pack_tall(pb[3, low, :] + unpack_tall(rx.at[1], 128, 1024), sx.at[5])
     send_x(5, LEFT)
+    turn(0)
+    turn(1)
     ring[2].wait_recv()
     pb[0, low, :] += unpack_tall(rx.at[2], 128, 1024)
     ring[3].wait_recv()
@@ -239,6 +249,8 @@
         picks.append(jnp.sum(jnp.where(hot, logit, 0.0), axis=1, keepdims=True))
         e = jnp.exp(logit - m)
         eb[0, half, :] = e.astype(BF16)
+        gall[0, half, :] = jnp.where(hot, 0.0, e).astype(BF16)
+        hot0[half, :] = hot.astype(F32).astype(BF16)
         pb[0, half, :] = e
         tops.append(m)
         sums.append(jnp.sum(e, axis=1, keepdims=True))
@@ -276,26 +288,26 @@
         st[out, 0, 2:3, :] = q
         return m, s, q
 
-    def turn(h):
+    def row_product(lhs, out):
         def step(n, carry):
-            at = pl.ds(pl.multiple_of(n * 256, 256), 256)
-            wt[h, :, at] = wbuf[h, at, :].T
+            at = pl.ds(pl.multiple_of((n % 4) * 256, 256), 256)
+            to = pl.ds(pl.multiple_of(n * 256, 256), 256)
+            res = jnp.dot(lhs[...], wt[n // 4, :, at], preferred_element_type=F32)
+            out[:, :, :, to] = res.reshape(NZ, 2, 16, 256)
             return carry
 
-        lax.fori_loop(0, 4, step, 0)
-
-    told = tell(0, [dev(core=oc)])
+        lax.fori_loop(0, 8, step, 0)
+
+    told = tell(0, [dev(core=oc)] + [dev(dy=k, core=cc) for k in (1, 2, 3) for cc in (c, oc)])
+    row_product(hot0, vt)
     join(0, told, 1)
     told = tell(1, [dev(dz=k) for k in range(1, NZ)])
-    turn(0)
-    join(1, told, 2)
-    told = tell(2, [dev(dy=k) for k in (1, 2, 3)])
-    turn(1)
-    m, s, q = join(2, told, 3)
+    row_product(gall.at[0], gt.at[0])
+    m, s, q = join(1, told, 2)
     loss[...] = m + jnp.log(s) - q
     weigh = cot[...]
     fx[0, 0:1, :] = weigh * (jnp.exp(st[0, 0, 0:1, :] - m) / s)
-    fx[0, 1:2, :] = weigh * (jnp.exp(q - m) / s - 1.0)
+    fx[0, 1:2, :] = (weigh * (jnp.exp(q - m) / s - 1.0)).astype(BF16).astype(F32)
     fx[0, 2:3, :] = tgt[...].astype(F32)
     line = {}
     for k in (1, 3, 2):
@@ -315,22 +327,33 @@
 
     pair, zd = {}, {}
 
-    def block_product(*blocks):
+    def send_pair(r, h):
+        cols = pl.ds(h * 1024, 1024)
+        d = remote(gt.at[r, :, oc, :, cols], rb.at[r, :, :, cols], ds_.at[r, h], dr.at[r, h], dev(core=oc))
+        d.start()
+        pair[r, h] = d
+        sent.append(d)
+
+    def block_product(h, *blocks):
         def step(n, carry):
-            at = pl.ds(pl.multiple_of((n % 4) * 256, 256), 256)
-            out = pl.ds(pl.multiple_of(n * 256, 256), 256)
+            at = pl.ds(pl.multiple_of(n * 256, 256), 256)
+            out = pl.ds(pl.multiple_of(n * 256 + h * 1024, 256), 256)
             lhs = jnp.concatenate([gall[r] for r in blocks], axis=0)
-            res = jnp.dot(lhs, wt[n // 4, :, at], preferred_element_type=F32)
+            res = jnp.dot(lhs, wt[h, :, at], preferred_element_type=F32)
             for i, r in enumerate(blocks):
                 gt[r, :, :, :, out] = res[i * 256 : (i + 1) * 256].reshape(NZ, 2, 16, 256)
             return carry
 
-        lax.fori_loop(0, 8, step, 0)
+        lax.fori_loop(0, 4, step, 0)
         for r in blocks:
-            d = remote(gt.at[r, :, oc], rb.at[r], ds_.at[r], dr.at[r], dev(core=oc))
-            d.start()
-            pair[r] = d
-            sent.append(d)
+            send_pair(r, h)
+
+    def own_block(h):
+        factor, at_target = (as_column(fx[0, i : i + 1, :]).reshape(NZ, 2, 16, 1) for i in range(2))
+        for j in range(h * 4, h * 4 + 4):
+            cols = slice(j * 256, j * 256 + 256)
+            gt[0, :, :, :, cols] = gt[0, :, :, :, cols] * factor + vt[:, :, :, cols] * at_target
+        send_pair(0, h)
 
     def z_half(r, k, d, half):
         zz = (z + (4 - k if d == 0 else 4 + k)) % NZ
@@ -351,10 +374,10 @@
         sent.append(cp)
 
     def z_step(r, k):
-        if k == 0:
-            pair[r].wait_recv()
         if k < 4:
             for d in range(2):
+                if k == 0:
+                    pair[r, d].wait_recv()
                 z_half(r, k, d, d)
         if k < 3:
             for d in range(2):
@@ -377,40 +400,45 @@
     f0 = send_e(4, 3, 2, upper, RIGHT)
     b0.wait_recv()
     f1 = send_e(5, 1, 2, lower, LEFT)
+    own_block(0)
+    own_block(1)
     scale(0)
-    block_product(0)
     z_step(0, 0)
     a1.wait_recv()
     scale(3)
     b1.wait_recv()
     scale(1)
-    block_product(3, 1)
+    block_product(0, 3, 1)
     z_step(0, 1)
+    block_product(1, 3, 1)
     f0.wait_recv()
     f1.wait_recv()
     scale(2)
+    block_product(0, 2)
+    z_step(0, 2)
     z_step(3, 0)
-    block_product(2)
     z_step(1, 0)
-    z_step(0, 2)
+    block_product(1, 2)
     z_step(2, 0)
+    z_step(0, 3)
     z_step(3, 1)
     z_step(1, 1)
-    z_step(0, 3)
+    z_step(0, 4)
+    weight_tile(0)
     z_step(2, 1)
+    weight_tile(1)
     z_step(3, 2)
+    weight_tile(2)
     z_step(1, 2)
-    z_step(0, 4)
+    weight_tile(3)
     z_step(2, 2)
     z_step(3, 3)
+    weight_tile(4)
     z_step(1, 3)
-    weight_tile(0)
     z_step(2, 3)
+    weight_tile(5)
     z_step(3, 4)
-    weight_tile(1)
     z_step(1, 4)
-    weight_tile(2)
-    weight_tile(3)
     z_step(2, 4)
 
     def held(k):
@@ -423,8 +451,6 @@
         d.start()
         sent.append(d)
         home.append((k, d))
-    weight_tile(4)
-    weight_tile(5)
     weight_tile(6)
     weight_tile(7)
     total = held(0)
@@ -450,6 +476,7 @@
 
 
 def shards(hidden, weight, targets, cotangent):
+    args = (hidden, weight, targets.reshape(1, 256), cotangent.reshape(1, 256))
     vm, dma = pltpu.VMEM, pltpu.SemaphoreType.DMA
     space = pl.BlockSpec(memory_space=pltpu.VMEM)
     raw = pl.BlockSpec(memory_space=pl.ANY)
@@ -475,6 +502,8 @@
             vm((4, 256, 1024), BF16),
             vm((4, 8, 256), F32),
             vm((4, 256, 1024), BF16),
+            vm((256, 1024), BF16),
+            vm((NZ, 2, 16, 2048), F32),
             vm((4, NZ, 2, 16, 2048), F32),
             vm((4, NZ, 16, 2048), F32),
             vm((4, 2, 4, 2, 144, 128), I16),
@@ -482,14 +511,14 @@
             vm((4, 16, 2048), F32),
             vm((4, 272, 128), I16),
             vm((4, 272, 128), I16),
-            dma((6,)), dma((4, 8)), dma((4, 8)), dma((6,)), dma((6,)),
-            dma((3, 8)), dma((3, 8)), dma((6,)), dma((6,)), dma((4,)), dma((4,)), dma((4,)), dma((4,)),
+            dma((6,)), dma((13,)), dma((13,)), dma((6,)), dma((6,)),
+            dma((2, 8)), dma((2, 8)), dma((6,)), dma((6,)), dma((4,)), dma((4,)), dma((4, 2)), dma((4, 2)),
             dma((4, 2, 4, 2)), dma((4, 2, 4, 2)), dma((4,)), dma((4,)),
         ],
         compiler_params=pltpu.CompilerParams(
-            collective_id=0, has_side_effects=True, vmem_limit_bytes=46 * 1024 * 1024
+            collective_id=0, has_side_effects=True, vmem_limit_bytes=49 * 1024 * 1024
         ),
-    )(hidden, weight, targets.reshape(1, 256), cotangent.reshape(1, 256))
+    )(*(pltpu.with_memory_space_constraint(a, pltpu.HBM) for a in args))
     loss, gh, gw = pl.pallas_call(
         finish,
         out_shape=(

time: 106 us -> 102 us (0.962)
  Pallas kernels: 104 us -> 102 us
  local copies, waits for them, and re-layouts: 1.35 us -> 0 us
    pallas_call x1, Pallas kernels: 102 us -> 99.5 us  [shards(): pl.pallas_call(kernel, out_shape=(jax.ShapeDtypeStruct((1, 256), F32), ja...]
    unnamed x4 -> x0, local copies, waits for them, and re-layouts: 1.35 us -> none
where the time goes in v3:
time: 102 us
  Pallas kernels  102 us (100%)
    pallas_call x1, Pallas kernels, shards(): pl.pallas_call(kernel, out_shape=(jax.ShapeDtypeStruct((1, 256), F32), ja...  99.5 us
    pallas_call x1, Pallas kernels, shards(): pl.pallas_call(finish, out_shape=(jax.ShapeDtypeStruct((1, 256), F32), ja...  2.04 us

profile of v3, /device:TPU:1, one launch (start us, length us, event | category | flops | bytes accessed | tf_op | source)
XLA Modules:
  0.0 102.4 jit_solution(3433825158911660101)
XLA Ops:
  0.6 99.5 %shard_map.67 = (f32[1,256]{1,0:T(1,128)S(1)}, bf16[16,2048]{1,0:T(8,128)(2,1)S(1)}, bf16[2048,1024]{1,0:T(8,128)(2,1)S(1)}) custom-call(bf16[256,8192]{1,0:T(8,128)(2,1)} %hid.1, bf16[2048,1024]{1,0:T(8,128)(2,1)} %w.1, s32[1,256]{1,0:T(1,128)} %bitcast.3, f32[1,256]{1,0:T(1,128)} %bitcast.4), custom_call_target="tpu_custom_call" | custom-call | tf_op jit(solution)/shard_map/pallas_call | solution.py:483
  100.2 2.0 %shard_map.68 = (f32[1,256]{1,0:T(1,128)}, bf16[16,2048]{1,0:T(8,128)(2,1)}, bf16[2048,1024]{1,0:T(8,128)(2,1)}) custom-call(f32[1,256]{1,0:T(1,128)S(1)} %get-tuple-element.9.loss_in, bf16[16,2048]{1,0:T(8,128)(2,1)S(1)} %get-tuple-element.10.gh_in, bf16[2048,1024]{1,0:T(8,128)(2,1)S(1)} %get-tuple-element.11.gw_in), custom_call_target="tpu_custom_call" | custom-call | tf_op jit(solution)/shard_map/pallas_call | solution.py:522

commit v4 on v3

--- a/solution.py
+++ b/solution.py
@@ -65,7 +65,7 @@
 
 def kernel(
     hid, w, tgt_in, cot_in, loss, gh, gw,
-    tgt, cot,    hbuf, wbuf, wt, pb, sx, rx, st, eb, fx, gall, hot0, vt, gt, rb, zs, zr, fin, ys, yr,
+    tgt, cot, xh,     hbuf, wbuf, wt, pb, sx, rx, st, eb, fx, gall, hot0, vt, gt, rb, zs, zr, fin, ys, yr,
     lsem, hs, hr, xs, xr, ss, sr, gs, gr, fs, fr, ds_, dr, zss, zrs, yss, yrs,
 ):
     x = lax.axis_index("dp")
@@ -83,6 +83,15 @@
             src_ref=src, dst_ref=dst, send_sem=send, recv_sem=recv,
             device_id=to, device_id_type=pl.DeviceIdType.MESH,
         )
+
+    def columns_for(r):
+        to = (4 - r) % 4
+        return to, pl.ds(pl.multiple_of(((x + to) % NX) * 2048 + c * 1024, 1024), 1024)
+
+    mine = pl.ds(pl.multiple_of(y * 64, 64), 64)
+    far_to, far_cols = columns_for(2)
+    ahead = pltpu.make_async_copy(hid.at[mine, far_cols], xh, lsem.at[6])
+    ahead.start()
 
     local = [pltpu.make_async_copy(w.at[pl.ds(h * 1024, 1024), :], wbuf.at[h], lsem.at[h]) for h in range(2)]
     for h in range(2):
@@ -101,14 +110,9 @@
     pl.semaphore_wait(barrier, len(peers))
 
     sent = []
-    mine = pl.ds(pl.multiple_of(y * 64, 64), 64)
     take = {}
-    def columns_for(r):
-        to = (4 - r) % 4
-        return to, pl.ds(pl.multiple_of(((x + to) % NX) * 2048 + c * 1024, 1024), 1024)
-
-    to, cols = columns_for(2)
-    take[2] = remote(hid.at[mine, cols], hbuf.at[c, 2, mine, :], hs.at[0], hr.at[0], dev(dx=to))
+    ahead.wait()
+    take[2] = remote(xh, hbuf.at[c, 2, mine, :], hs.at[0], hr.at[0], dev(dx=far_to))
     take[2].start()
     sent.append(take[2])
 
@@ -355,23 +359,25 @@
             gt[0, :, :, :, cols] = gt[0, :, :, :, cols] * factor + vt[:, :, :, cols] * at_target
         send_pair(0, h)
 
+    def slot(k, half):
+        return 2 * k - 1 + half if k else 0
+
     def z_half(r, k, d, half):
         zz = (z + (4 - k if d == 0 else 4 + k)) % NZ
         cols = pl.ds(half * 1024, 1024)
         val = gt[r, zz, c, :, cols] + rb[r, zz, :, cols]
         if k > 1 or (k == 1 and half == d):
             zd[r, d, k - 1, half].wait_recv()
-            val = val + unpack_flat(zr.at[r, d, k - 1, half], 16, 1024)
+            val = val + unpack_flat(zr.at[r, d, slot(k - 1, half)], 16, 1024)
         if k == 4:
             return val
-        pack_flat(val, zs.at[r, d, k, half])
+        at = slot(k, half)
+        pack_flat(val, zs.at[r, d, at])
         cp = remote(
-            zs.at[r, d, k, half], zr.at[r, d, k, half],
-            zss.at[r, d, k, half], zrs.at[r, d, k, half], dev(dz=1 if d == 0 else -1),
+            zs.at[r, d, at], zr.at[r, d, at], zss.at[0], zrs.at[r, d, at], dev(dz=1 if d == 0 else -1)
         )
         cp.start()
         zd[r, d, k, half] = cp
-        sent.append(cp)
 
     def z_step(r, k):
         if k < 4:
@@ -387,7 +393,7 @@
                 other = zd[r, 1, 3, half]
                 val = z_half(r, 4, 0, half)
                 other.wait_recv()
-                fin[r, :, half * 1024 : half * 1024 + 1024] = val + unpack_flat(zr.at[r, 1, 3, half], 16, 1024)
+                fin[r, :, half * 1024 : half * 1024 + 1024] = val + unpack_flat(zr.at[r, 1, slot(3, half)], 16, 1024)
 
     def weight_tile(f):
         h, at = f // 4, pl.ds((f % 4) * 256, 256)
@@ -415,28 +421,25 @@
     f1.wait_recv()
     scale(2)
     block_product(0, 2)
-    z_step(0, 2)
     z_step(3, 0)
     z_step(1, 0)
     block_product(1, 2)
+    z_step(0, 2)
     z_step(2, 0)
-    z_step(0, 3)
     z_step(3, 1)
     z_step(1, 1)
+    z_step(0, 3)
+    z_step(2, 1)
+    z_step(3, 2)
+    weight_tile(0)
+    z_step(1, 2)
     z_step(0, 4)
-    weight_tile(0)
-    z_step(2, 1)
-    weight_tile(1)
-    z_step(3, 2)
-    weight_tile(2)
-    z_step(1, 2)
-    weight_tile(3)
     z_step(2, 2)
     z_step(3, 3)
-    weight_tile(4)
+    weight_tile(1)
     z_step(1, 3)
     z_step(2, 3)
-    weight_tile(5)
+    weight_tile(2)
     z_step(3, 4)
     z_step(1, 4)
     z_step(2, 4)
@@ -451,6 +454,9 @@
         d.start()
         sent.append(d)
         home.append((k, d))
+    weight_tile(3)
+    weight_tile(4)
+    weight_tile(5)
     weight_tile(6)
     weight_tile(7)
     total = held(0)
@@ -462,6 +468,7 @@
     def drain():
         for d in sent:
             d.wait_send()
+        remote(zs, zr, zss.at[0], zrs.at[0, 0, 0], dev(dz=1)).wait_send()
 
     drain()
 
@@ -492,6 +499,7 @@
         scratch_shapes=[
             vm((1, 256), jnp.int32),
             vm((1, 256), F32),
+            vm((64, 1024), BF16),
             vm((2, 4, 256, 1024), BF16),
             vm((2, 1024, 1024), BF16),
             vm((2, 1024, 1024), BF16),
@@ -506,14 +514,14 @@
             vm((NZ, 2, 16, 2048), F32),
             vm((4, NZ, 2, 16, 2048), F32),
             vm((4, NZ, 16, 2048), F32),
-            vm((4, 2, 4, 2, 144, 128), I16),
-            vm((4, 2, 4, 2, 144, 128), I16),
+            vm((4, 2, 7, 144, 128), I16),
+            vm((4, 2, 7, 144, 128), I16),
             vm((4, 16, 2048), F32),
             vm((4, 272, 128), I16),
             vm((4, 272, 128), I16),
-            dma((6,)), dma((13,)), dma((13,)), dma((6,)), dma((6,)),
+            dma((7,)), dma((13,)), dma((13,)), dma((6,)), dma((6,)),
             dma((2, 8)), dma((2, 8)), dma((6,)), dma((6,)), dma((4,)), dma((4,)), dma((4, 2)), dma((4, 2)),
-            dma((4, 2, 4, 2)), dma((4, 2, 4, 2)), dma((4,)), dma((4,)),
+            dma((1,)), dma((4, 2, 7)), dma((4,)), dma((4,)),
         ],
         compiler_params=pltpu.CompilerParams(
             collective_id=0, has_side_effects=True, vmem_limit_bytes=49 * 1024 * 1024

time: 102 us -> 101 us (level)
  Pallas kernels: 102 us -> 99.7 us
    pallas_call x1, Pallas kernels: 99.5 us -> 97.7 us  [shards(): pl.pallas_call(kernel, out_shape=(jax.ShapeDtypeStruct((1, 256), F32), ja...]
where the time goes in v4:
time: 101 us
  Pallas kernels  99.7 us (99%)
    pallas_call x1, Pallas kernels, shards(): pl.pallas_call(kernel, out_shape=(jax.ShapeDtypeStruct((1, 256), F32), ja...  97.7 us
    pallas_call x1, Pallas kernels, shards(): pl.pallas_call(finish, out_shape=(jax.ShapeDtypeStruct((1, 256), F32), ja...  2.04 us

profile of v4, /device:TPU:1, one launch (start us, length us, event | category | flops | bytes accessed | tf_op | source)
XLA Modules:
  0.0 100.5 jit_solution(1341164907657915663)
XLA Ops:
  0.6 97.7 %shard_map.67 = (f32[1,256]{1,0:T(1,128)S(1)}, bf16[16,2048]{1,0:T(8,128)(2,1)S(1)}, bf16[2048,1024]{1,0:T(8,128)(2,1)S(1)}) custom-call(bf16[256,8192]{1,0:T(8,128)(2,1)} %hid.1, bf16[2048,1024]{1,0:T(8,128)(2,1)} %w.1, s32[1,256]{1,0:T(1,128)} %bitcast.3, f32[1,256]{1,0:T(1,128)} %bitcast.4), custom_call_target="tpu_custom_call" | custom-call | tf_op jit(solution)/shard_map/pallas_call | solution.py:490
  98.3 2.0 %shard_map.68 = (f32[1,256]{1,0:T(1,128)}, bf16[16,2048]{1,0:T(8,128)(2,1)}, bf16[2048,1024]{1,0:T(8,128)(2,1)}) custom-call(f32[1,256]{1,0:T(1,128)S(1)} %get-tuple-element.9.loss_in, bf16[16,2048]{1,0:T(8,128)(2,1)S(1)} %get-tuple-element.10.gh_in, bf16[2048,1024]{1,0:T(8,128)(2,1)S(1)} %get-tuple-element.11.gw_in), custom_call_target="tpu_custom_call" | custom-call | tf_op jit(solution)/shard_map/pallas_call | solution.py:530

commit v5 on v4

--- a/solution.py
+++ b/solution.py
@@ -51,6 +51,22 @@
     return jnp.concatenate(
         [src[j * rows : (j + 1) * rows, :].astype(F32) * scale for j in range(cols // 128)], axis=1
     )
+
+
+def pack_half(x, dst):
+    k = row_code(x)
+    inv = jnp.exp(k * (-1.0 / FINE)) * TOP
+    for j in range(8):
+        dst[j * 16 : (j + 1) * 16, :] = jnp.round(x[:, j * 128 : (j + 1) * 128] * inv).astype(I16)
+    lower = lax.broadcasted_iota(jnp.int32, (8, 128), 1) < 64
+    dst[128:136, :] = jnp.where(lower, k[:8], k[8:]).astype(I16)
+
+
+def unpack_half(src):
+    k = src[128:136, :].astype(F32)
+    k = jnp.concatenate([k[:, 0:1], k[:, 64:65]], axis=0)
+    scale = jnp.exp(k * (1.0 / FINE)) * (1.0 / TOP)
+    return jnp.concatenate([src[j * 16 : (j + 1) * 16, :].astype(F32) * scale for j in range(8)], axis=1)
 
 
 def as_column(line):
@@ -246,6 +262,7 @@
 
     upper, lower = pl.ds(0, 128), pl.ds(128, 128)
     tops, sums, picks = [], [], []
+    first_sends = []
     for half in (top, low):
         logit = pb[0, half, :]
         m = jnp.max(logit, axis=1, keepdims=True)
@@ -258,8 +275,8 @@
         pb[0, half, :] = e
         tops.append(m)
         sums.append(jnp.sum(e, axis=1, keepdims=True))
-    a0 = send_e(0, 0, 3, upper, RIGHT)
-    b0 = send_e(1, 0, 1, lower, LEFT)
+        first_sends.append(send_e(0, 0, 3, upper, RIGHT) if half is top else send_e(1, 0, 1, lower, LEFT))
+    a0, b0 = first_sends
     a1 = send_e(2, 0, 3, lower, RIGHT)
     b1 = send_e(3, 0, 1, upper, LEFT)
     st[0, 0, 0:1, :] = as_line(jnp.concatenate(tops, axis=0))
@@ -368,11 +385,11 @@
         val = gt[r, zz, c, :, cols] + rb[r, zz, :, cols]
         if k > 1 or (k == 1 and half == d):
             zd[r, d, k - 1, half].wait_recv()
-            val = val + unpack_flat(zr.at[r, d, slot(k - 1, half)], 16, 1024)
+            val = val + unpack_half(zr.at[r, d, slot(k - 1, half)])
         if k == 4:
             return val
         at = slot(k, half)
-        pack_flat(val, zs.at[r, d, at])
+        pack_half(val, zs.at[r, d, at])
         cp = remote(
             zs.at[r, d, at], zr.at[r, d, at], zss.at[0], zrs.at[r, d, at], dev(dz=1 if d == 0 else -1)
         )
@@ -393,7 +410,7 @@
                 other = zd[r, 1, 3, half]
                 val = z_half(r, 4, 0, half)
                 other.wait_recv()
-                fin[r, :, half * 1024 : half * 1024 + 1024] = val + unpack_flat(zr.at[r, 1, slot(3, half)], 16, 1024)
+                fin[r, :, half * 1024 : half * 1024 + 1024] = val + unpack_half(zr.at[r, 1, slot(3, half)])
 
     def weight_tile(f):
         h, at = f // 4, pl.ds((f % 4) * 256, 256)
@@ -514,8 +531,8 @@
             vm((NZ, 2, 16, 2048), F32),
             vm((4, NZ, 2, 16, 2048), F32),
             vm((4, NZ, 16, 2048), F32),
-            vm((4, 2, 7, 144, 128), I16),
-            vm((4, 2, 7, 144, 128), I16),
+            vm((4, 2, 7, 136, 128), I16),
+            vm((4, 2, 7, 136, 128), I16),
             vm((4, 16, 2048), F32),
             vm((4, 272, 128), I16),
             vm((4, 272, 128), I16),

time: 101 us -> 99.6 us (0.986)
  no operation moved by 1% of the time
where the time goes in v5:
time: 99.6 us; the launch traced here: 99.5 us
  Pallas kernels  98.7 us (99%)
    pallas_call x1, Pallas kernels, shards(): pl.pallas_call(kernel, out_shape=(jax.ShapeDtypeStruct((1, 256), F32), ja...  96.7 us
    pallas_call x1, Pallas kernels, shards(): pl.pallas_call(finish, out_shape=(jax.ShapeDtypeStruct((1, 256), F32), ja...  2.04 us

profile of v5, /device:TPU:1, one launch (start us, length us, event | category | flops | bytes accessed | tf_op | source)
XLA Modules:
  0.0 99.5 jit_solution(12607241554750792201)
XLA Ops:
  0.6 96.7 %shard_map.67 = (f32[1,256]{1,0:T(1,128)S(1)}, bf16[16,2048]{1,0:T(8,128)(2,1)S(1)}, bf16[2048,1024]{1,0:T(8,128)(2,1)S(1)}) custom-call(bf16[256,8192]{1,0:T(8,128)(2,1)} %hid.1, bf16[2048,1024]{1,0:T(8,128)(2,1)} %w.1, s32[1,256]{1,0:T(1,128)} %bitcast.3, f32[1,256]{1,0:T(1,128)} %bitcast.4), custom_call_target="tpu_custom_call" | custom-call | tf_op jit(solution)/shard_map/pallas_call | solution.py:507
  97.3 2.0 %shard_map.68 = (f32[1,256]{1,0:T(1,128)}, bf16[16,2048]{1,0:T(8,128)(2,1)}, bf16[2048,1024]{1,0:T(8,128)(2,1)}) custom-call(f32[1,256]{1,0:T(1,128)S(1)} %get-tuple-element.9.loss_in, bf16[16,2048]{1,0:T(8,128)(2,1)S(1)} %get-tuple-element.10.gh_in, bf16[2048,1024]{1,0:T(8,128)(2,1)S(1)} %get-tuple-element.11.gw_in), custom_call_target="tpu_custom_call" | custom-call | tf_op jit(solution)/shard_map/pallas_call | solution.py:547

commit v6 on v5

--- a/solution.py
+++ b/solution.py
@@ -199,10 +199,9 @@
     ring = {}
 
     def send_x(k, dx):
-        d = remote(sx.at[k], rx.at[k], xs.at[k], xr.at[k], dev(dx=dx))
+        d = remote(sx.at[k], rx.at[k], xs.at[0], xr.at[k], dev(dx=dx))
         d.start()
         ring[k] = d
-        sent.append(d)
 
     top, low = slice(0, 128), slice(128, 256)
     spread()
@@ -255,9 +254,8 @@
     lanes = lax.broadcasted_iota(jnp.int32, (128, 1024), 1).astype(F32) + first
 
     def send_e(k, src, dst, half, dx):
-        d = remote(eb.at[src, half, :], eb.at[dst, half, :], gs.at[k], gr.at[k], dev(dx=dx))
-        d.start()
-        sent.append(d)
+        d = remote(eb.at[src, half, :], eb.at[dst, half, :], gs.at[0], gr.at[k], dev(dx=dx))
+        d.start()
         return d
 
     upper, lower = pl.ds(0, 128), pl.ds(128, 128)
@@ -286,9 +284,8 @@
     def tell(level, places):
         out = []
         for k, p in enumerate(places, 1):
-            d = remote(st.at[level, 0], st.at[level, k], ss.at[level, k], sr.at[level, k], p)
+            d = remote(st.at[level, 0], st.at[level, k], ss.at[0], sr.at[level, k], p)
             d.start()
-            sent.append(d)
             out.append(d)
         return out
 
@@ -350,10 +347,9 @@
 
     def send_pair(r, h):
         cols = pl.ds(h * 1024, 1024)
-        d = remote(gt.at[r, :, oc, :, cols], rb.at[r, :, :, cols], ds_.at[r, h], dr.at[r, h], dev(core=oc))
+        d = remote(gt.at[r, :, oc, :, cols], rb.at[r, :, :, cols], ds_.at[0], dr.at[r, h], dev(core=oc))
         d.start()
         pair[r, h] = d
-        sent.append(d)
 
     def block_product(h, *blocks):
         def step(n, carry):
@@ -486,6 +482,12 @@
         for d in sent:
             d.wait_send()
         remote(zs, zr, zss.at[0], zrs.at[0, 0, 0], dev(dz=1)).wait_send()
+        remote(rb, rb, ds_.at[0], dr.at[0, 0], dev(core=oc)).wait_send()
+        remote(sx, rx, xs.at[0], xr.at[0], dev(dx=1)).wait_send()
+        stats = st.at[pl.ds(0, 2), pl.ds(0, 7)]
+        remote(stats, stats, ss.at[0], sr.at[0, 0], dev(dz=1)).wait_send()
+        three = eb.at[pl.ds(0, 3)]
+        remote(three, three, gs.at[0], gr.at[0], dev(dx=1)).wait_send()
 
     drain()
 
@@ -536,8 +538,8 @@
             vm((4, 16, 2048), F32),
             vm((4, 272, 128), I16),
             vm((4, 272, 128), I16),
-            dma((7,)), dma((13,)), dma((13,)), dma((6,)), dma((6,)),
-            dma((2, 8)), dma((2, 8)), dma((6,)), dma((6,)), dma((4,)), dma((4,)), dma((4, 2)), dma((4, 2)),
+            dma((7,)), dma((13,)), dma((13,)), dma((1,)), dma((6,)),
+            dma((1,)), dma((2, 8)), dma((1,)), dma((6,)), dma((4,)), dma((4,)), dma((1,)), dma((4, 2)),
             dma((1,)), dma((4, 2, 7)), dma((4,)), dma((4,)),
         ],
         compiler_params=pltpu.CompilerParams(

time: 99.6 us -> 99.3 us (level)
  no operation moved by 1% of the time
where the time goes in v6:
time: 99.3 us; the launch traced here: 99.2 us
  Pallas kernels  98.4 us (99%)
    pallas_call x1, Pallas kernels, shards(): pl.pallas_call(kernel, out_shape=(jax.ShapeDtypeStruct((1, 256), F32), ja...  96.3 us
    pallas_call x1, Pallas kernels, shards(): pl.pallas_call(finish, out_shape=(jax.ShapeDtypeStruct((1, 256), F32), ja...  2.04 us

profile of v6, /device:TPU:1, one launch (start us, length us, event | category | flops | bytes accessed | tf_op | source)
XLA Modules:
  0.0 99.2 jit_solution(15632275471986089220)
XLA Ops:
  0.6 96.3 %shard_map.67 = (f32[1,256]{1,0:T(1,128)S(1)}, bf16[16,2048]{1,0:T(8,128)(2,1)S(1)}, bf16[2048,1024]{1,0:T(8,128)(2,1)S(1)}) custom-call(bf16[256,8192]{1,0:T(8,128)(2,1)} %hid.1, bf16[2048,1024]{1,0:T(8,128)(2,1)} %w.1, s32[1,256]{1,0:T(1,128)} %bitcast.3, f32[1,256]{1,0:T(1,128)} %bitcast.4), custom_call_target="tpu_custom_call" | custom-call | tf_op jit(solution)/shard_map/pallas_call | solution.py:509
  97.0 2.0 %shard_map.68 = (f32[1,256]{1,0:T(1,128)}, bf16[16,2048]{1,0:T(8,128)(2,1)}, bf16[2048,1024]{1,0:T(8,128)(2,1)}) custom-call(f32[1,256]{1,0:T(1,128)S(1)} %get-tuple-element.9.loss_in, bf16[16,2048]{1,0:T(8,128)(2,1)S(1)} %get-tuple-element.10.gh_in, bf16[2048,1024]{1,0:T(8,128)(2,1)S(1)} %get-tuple-element.11.gw_in), custom_call_target="tpu_custom_call" | custom-call | tf_op jit(solution)/shard_map/pallas_call | solution.py:549
